TPU v7x, 256 devices: a whole 4x4x8 slice. The times are simulated.
256 devices in a mesh: row: 16 (over y, x), col: 16 (over z, core).
Axes of the slice: x: 4, y: 4, z: 8, core: 2. Of those that a mesh axis runs over, the one named last changes fastest.
Arguments:
- trail: float32 [2, 16, 512, 2, 16, 512], P(None, 'row', None, None, 'col'), may hold values from -6 to 6
- panel: float32 [2, 16, 512, 512], P(None, 'row', None, 'col'), may hold values from -6 to 6
- row_basis: float32 [2, 16, 64, 512], P(None, 'row', None, 'col'), may hold values from -0.75 to 0.75
- row_coeff: float32 [2, 16, 64, 512], P(None, 'row', None, 'col'), may hold values from -0.25 to 0.25
- col_basis: float32 [2, 16, 64, 512], P(None, 'col', None, 'row'), may hold values from -0.75 to 0.75
- col_scaled: float32 [2, 16, 64, 512], P(None, 'col', None, 'row'), may hold values from -0.25 to 0.25
- pivot_basis: float32 [64, 512], P(None, 'col'), may hold values from -0.75 to 0.75
- pivot_scaled: float32 [64, 512], replicated, may hold values from -0.25 to 0.25
- sketch: float32 [64, 512], replicated, may hold values from -6 to 6
- perm: int32 [512], replicated, may hold values from 0 to 511, each once
- pair_kind: int32 [256], replicated, may hold values from 0 to 1
- pivot_values: float32 [3, 256], replicated, may hold values from -3 to 3, as said below
Outputs:
- trail_out: float32 [2, 16, 512, 2, 16, 512], P(None, 'row', None, None, 'col')
- basis_out: float32 [2, 16, 64, 512], P(None, 'row')
- coeff_out: float32 [2, 16, 64, 512], P(None, 'row')
Inputs may be any that keep to these rules, and one draw needn't show every extreme that they name: `pivot_values`: rows 0 and 1 have magnitudes between 0.5 and 0.7; row 2 has magnitude 1.2 or more.
All inputs are finite; a program needn't handle non-finite values.
Results may differ from a plain program's by a relative error of at most 0.00013.
Values sent between devices are 32-bit elements; how exact they have to be, the bound alone decides.
A program may use at most 64 MiB of HBM per device.

v0:
```python
import jax
import jax.numpy as jnp
from jax import lax
from jax.sharding import PartitionSpec as P


def gather_turned(arrays, axis, dims):
    turned = [jnp.moveaxis(a, dim, 0) for a, dim in zip(arrays, dims)]
    both = jnp.concatenate([t.reshape(len(t), -1) for t in turned], axis=1)
    filled, at, outs = (lax.all_gather(both, axis, axis=0, tiled=True), 0, [])
    for t, dim in zip(turned, dims):
        share = filled[:, at : at + t[0].size].reshape(-1, *t.shape[1:])
        outs.append(jnp.moveaxis(share, 0, dim))
        at += t[0].size
    return tuple(outs)


def total_of_pieces(array, axis):
    return lax.all_gather(array, axis).sum(0)


def pair_apply(rows, pair_kind, pivot_values):
    shaped = rows.reshape(rows.shape[:-1] + (rows.shape[-1] // 2, 2))
    first_in = shaped[..., 0]
    second_in = shaped[..., 1]
    diag_one = pivot_values[0]
    diag_two = pivot_values[1]
    offdiag = pivot_values[2]
    determinant = diag_one * diag_two - offdiag * offdiag
    twin = pair_kind == 1
    first = jnp.where(
        twin, (first_in * diag_two - second_in * offdiag) / determinant, first_in / diag_one
    )
    second = jnp.where(
        twin, (second_in * diag_one - first_in * offdiag) / determinant, second_in / diag_two
    )
    return jnp.stack([first, second], axis=-1).reshape(rows.shape)


def tri_solve(lower, rhs):
    return jax.vmap(lambda low, right: jax.scipy.linalg.solve_triangular(low, right, lower=True))(
        lower, rhs
    )


def body(
    trail,
    panel,
    row_basis,
    row_coeff,
    col_basis,
    col_scaled,
    pivot_basis,
    pivot_scaled,
    sketch,
    perm,
    pair_kind,
    pivot_values,
):
    highest = lax.Precision.HIGHEST
    width = sketch.shape[1]
    block = panel.shape[3]
    xrows, yrows = gather_turned((row_basis, row_coeff), "col", (3, 3))
    zcols, gcols = gather_turned((col_basis, col_scaled), "row", (3, 3))
    xrows = xrows[:, 0]
    yrows = yrows[:, 0]
    zcols = zcols[:, 0]
    gcols = gcols[:, 0]
    core = jnp.einsum("arp,bsp->arbs", yrows, gcols, precision=highest)
    left = jnp.einsum("arp,arbs->apbs", xrows, core, precision=highest)
    change = jnp.einsum("apbs,bsq->apbq", left, zcols, precision=highest)
    trail_out = trail - change[:, None, :, :, None, :]
    pcore = jnp.einsum("arp,sp->ars", yrows, pivot_scaled, precision=highest)
    pleft = jnp.einsum("arp,ars->aps", xrows, pcore, precision=highest)
    updated = panel[:, 0] - jnp.einsum("aps,sq->apq", pleft, pivot_basis, precision=highest)
    scaled_t = pair_apply(sketch, pair_kind, pivot_values)
    column_ids = lax.axis_index("col") * block + jnp.arange(block, dtype=jnp.int32)
    selector = (perm[:, None] == column_ids[None, :]).astype(jnp.float32)
    local_sketch = jnp.dot(scaled_t, selector, precision=highest)
    partial_range = jnp.einsum("apq,rq->arp", updated, local_sketch, precision=highest)
    range_t = total_of_pieces(partial_range, "col")
    gram = jnp.einsum("arp,asp->ars", range_t, range_t, precision=highest) / width
    basis = tri_solve(jnp.linalg.cholesky(gram), range_t)
    projected_part = jnp.einsum("arp,apq->arq", basis, updated, precision=highest)
    projected = lax.all_gather(projected_part, "col", axis=2, tiled=True)
    permuted = jnp.take(projected, perm, axis=2)
    coeff = pair_apply(permuted, pair_kind, pivot_values) / jnp.sqrt(jnp.float32(width))
    return (trail_out, basis[:, None], coeff[:, None])


def solution(mesh):
    return jax.shard_map(
        body,
        mesh=mesh,
        in_specs=(
            P(None, "row", None, None, "col", None),
            P(None, "row", None, "col"),
            P(None, "row", None, "col"),
            P(None, "row", None, "col"),
            P(None, "col", None, "row"),
            P(None, "col", None, "row"),
            P(None, "col"),
            P(),
            P(),
            P(),
            P(),
            P(),
        ),
        out_specs=(
            P(None, "row", None, None, "col", None),
            P(None, "row", None, None),
            P(None, "row", None, None),
        ),
        check_vma=False,
    )
```

profile of v0, /device:TPU:1, one launch (start us, length us, event | category | flops | bytes accessed | tf_op | source)
XLA Modules:
  0.0 150.3 jit_solution(10058551639044590301)
XLA Ops:
  7.2 0.0 copy-start
  7.2 0.0 copy-start.5
  7.2 0.0 copy-start.6
  7.2 0.0 copy-start.2
  7.2 0.0 copy-start.3
  7.2 0.0 copy-start.4
  7.2 0.0 all-gather.3.cloned.1.call-start
  7.3 0.8 broadcast_compare_fusion
  8.0 0.8 fusion.11
  8.8 0.8 copy.78
  9.6 0.1 reshape.159
  9.7 0.8 copy.79
  10.5 0.1 reshape.160
  10.6 1.0 copy.85
  11.6 22.7 %all_gather.16 = f32[512,256]{1,0:T(8,128)S(1)} all-gather(f32[32,256]{1,0:T(8,128)S(1)} %pad_maximum_fusion.2), channel_id=1, replica_groups=mesh['row'=16,'col'=16] {'col'}, dimensions={0}, use_global_device_ids=true | all-gather | bytes 557056 | tf_op jit(solution)/shard_map/all_gather | solution.py:10
  34.4 0.1 copy.81
  34.6 0.1 copy.80
  34.7 2.2 %broadcast_select_fusion.3 = (f32[64,256,1]{0,2,1:T(1,128)S(1)}, f32[64,256,1]{0,2,1:T(1,128)S(1)}) fusion(pred[256]{0:T(512)(128)(4,1)S(1)} %broadcast_compare_fusion, f32[64,256,2]{0,2,1:T(2,128)S(1)} %bitcast.108, f32[256]{0:T(256)S(1)} %bitcast.120, f32[256]{0:T(256)S(1)} %bitcast.126, f32[256]{0:T(256)S(1)} %bitcast.123, f32[256]{0:T(256)S(1)} %bitcast.117), kind=kLoop, calls=%fused_computation.11 | loop fusion | flops 196608 | bytes 266496 | tf_op jit(solution)/shard_map/jit(_where)/select_n | solution.py:31
  36.9 0.3 pad_maximum_fusion
  37.2 0.0 copy-done
  37.2 0.5 fusion.1
  37.7 0.4 fusion.14
  38.1 0.0 copy-done.5
  38.1 0.4 convolution_bitcast_fusion.1
  38.5 0.0 copy-done.6
  38.5 0.0 copy-done.2
  38.5 0.3 convolution_subtract_fusion
  38.8 1.1 convolution_bitcast_fusion
  40.0 0.0 all-gather.3.cloned.1.call-update
  40.0 0.2 broadcast_in_dim.45
  40.2 0.0 copy-done.3
  40.2 0.1 reshape.156
  40.3 0.0 copy-done.4
  40.3 0.1 reshape.157
  40.4 19.9 %all_gather.15 = f32[512,256]{1,0:T(8,128)S(1)} all-gather(f32[32,256]{1,0:T(8,128)S(1)} %pad_maximum_fusion.1), channel_id=1, replica_groups=mesh['row'=16,'col'=16] {'row'}, dimensions={0}, use_global_device_ids=true | all-gather | bytes 557056 | tf_op jit(solution)/shard_map/all_gather | solution.py:10
  60.3 0.1 copy.82
  60.5 0.1 copy.77
  60.6 11.0 %copy.84 = f32[2,1,512,2,1,512]{2,5,0,3,4,1:T(8,128)} copy(f32[2,1,512,2,1,512]{5,4,3,2,1,0:T(1,128)} %param.12) | data formatting | bytes 8388608 | tf_op args[0]
  71.6 0.5 fusion.12
  72.1 0.6 fusion.13
  72.7 6.7 %bitcast_subtract_fusion = f32[2,1,512,2,1,512]{2,5,0,3,4,1:T(8,128)} fusion(f32[2,1,512,2,1,512]{2,5,0,3,4,1:T(8,128)} %copy.84, f32[2,64,512,1]{2,1,3,0:T(8,128)S(1)} %bitcast.109, f32[2,512,2,64]{1,3,0,2:T(8,128)S(1)} %fusion.13), kind=kOutput, calls=%fused_computation.1 | convolution fusion | flops 806354944 | bytes 9175040 | tf_op jit(solution)/shard_map/apbs,bsq->apbq/dot_general | solution.py:71
  79.4 10.9 %copy.91 = f32[2,1,512,2,1,512]{5,4,3,2,1,0:T(1,128)} copy(f32[2,1,512,2,1,512]{2,5,0,3,4,1:T(8,128)} %bitcast_subtract_fusion) | data formatting | bytes 8388608
  90.3 0.0 all-gather.3.cloned.1.call-done
  90.3 2.6 %reduce_sum.9 = f32[2,64,512]{2,1,0:T(8,128)S(1)} reduce(f32[16,2,64,512]{3,2,1,0:T(8,128)} %bitcast.101, f32[]{:T(128)} %constant.67.clone.1), dimensions={0}, to_apply=%region_0.1 | reduce | flops 983040 | bytes 4456452 | tf_op jit(solution)/shard_map/reduce_sum | solution.py:19
  93.0 0.4 fusion.15
  93.4 0.1 copy.87
  93.5 11.7 %custom-call.8 = f32[2,64,64]{2,1,0:T(8,128)S(1)} custom-call(f32[2,64,64]{2,1,0:T(8,128)S(1)} %fusion.7), custom_call_target="Cholesky" | custom-call | tf_op jit(solution)/shard_map/jit(cholesky)/cholesky | solution.py:83
  105.2 0.1 compare_reduce_fusion
  105.3 0.1 select_bitcast_fusion
  105.4 9.8 %custom-call.9 = f32[2,1,64,64]{2,3,1,0:T(8,128)S(1)} custom-call(f32[2,1,64,64]{3,2,1,0:T(8,128)S(1)} %select_bitcast_fusion), custom_call_target="InvertDiagBlocksLowerTriangular" | custom-call | tf_op jit(solution)/shard_map/vmap(jit(_solve_triangular))/triangular_solve | solution.py:41
  115.3 0.4 fusion.5
  115.7 0.0 copy-start.1
  115.7 0.3 fusion.16
  116.1 20.6 %all_gather.19 = f32[2,64,512]{1,2,0:T(8,128)S(1)} all-gather(f32[2,64,32]{1,2,0:T(8,128)S(1)} %fusion.16), channel_id=1, replica_groups=mesh['row'=16,'col'=16] {'col'}, dimensions={2}, use_global_device_ids=true | all-gather | bytes 278528 | tf_op jit(solution)/shard_map/all_gather | solution.py:85
  136.6 0.4 copy.89
  137.0 2.1 %gather_fusion = f32[512,2,64]{2,1,0:T(2,128)S(1)} fusion(f32[2,64,512]{1,0,2:T(2,128)S(1)} %copy.89, s32[1024]{0:T(1024)S(1)} %pad_clamp_fusion), kind=kCustom, calls=%fused_computation | custom fusion | bytes 526336 | tf_op jit(solution)/shard_map/jit(_take)/gather | solution.py:86
  139.1 0.6 copy_select_fusion
  139.8 2.2 %broadcast_select_fusion.1 = (f32[2,64,256,1]{1,3,2,0:T(1,128)S(1)}, f32[2,64,256,1]{1,3,2,0:T(1,128)S(1)}) fusion(pred[256]{0:T(512)(128)(4,1)S(1)} %broadcast_compare_fusion, f32[2,64,256,2]{1,3,2,0:T(2,128)S(1)} %copy_select_fusion, f32[256]{0:T(256)S(1)} %bitcast.122, f32[256]{0:T(256)S(1)} %multiply_subtract_fusion, f32[256]{0:T(256)S(1)} %bitcast.125, ...), kind=kLoop, calls=%fused_computation.8 | loop fusion | flops 393216 | bytes 528640 | tf_op jit(solution)/shard_map/jit(_where)/select_n | solution.py:31
  142.0 0.6 maximum_multiply_fusion
  142.6 0.9 copy.93
  143.5 0.0 copy-done.1
  (15 shorter events, 0.2 us)
Async XLA Ops:
  7.2 30.0 %copy-start = (f32[64,512]{1,0:T(8,128)S(1)}, f32[64,512]{1,0:T(8,128)}, u32[]{:S(2)}) copy-start(f32[64,512]{1,0:T(8,128)} %param.19) | copy-start | bytes 393220
  7.2 30.9 %copy-start.5 = (s32[512]{0:T(512)S(1)}, s32[512]{0:T(512)}, u32[]{:S(2)}) copy-start(s32[512]{0:T(512)} %param.21) | copy-start | bytes 6148
  7.2 31.3 %copy-start.6 = (f32[64,32]{0,1:T(8,128)S(1)}, f32[64,32]{0,1:T(8,128)}, u32[]{:S(2)}) copy-start(f32[64,32]{0,1:T(8,128)} %param.18) | copy-start | bytes 24580
  7.2 31.3 %copy-start.2 = (f32[2,1,512,32]{2,3,1,0:T(8,128)S(1)}, f32[2,1,512,32]{2,3,1,0:T(8,128)}, u32[]{:S(2)}) copy-start(f32[2,1,512,32]{2,3,1,0:T(8,128)} %param.13) | copy-start | bytes 393220
  7.2 33.0 %copy-start.3 = (f32[2,1,64,32]{2,3,1,0:T(8,128)S(1)}, f32[2,1,64,32]{2,3,1,0:T(8,128)}, u32[]{:S(2)}) copy-start(f32[2,1,64,32]{2,3,1,0:T(8,128)} %param.16) | copy-start | bytes 49156
  7.2 33.1 %copy-start.4 = (f32[2,1,64,32]{2,3,1,0:T(8,128)S(1)}, f32[2,1,64,32]{2,3,1,0:T(8,128)}, u32[]{:S(2)}) copy-start(f32[2,1,64,32]{2,3,1,0:T(8,128)} %param.17) | copy-start | bytes 49156
  7.2 83.1 %all-gather.3.cloned.1.call-start = ((), (), s32[]{:S(2)}) async-start(), calls=%async_computation | async-start | bytes 4456448 | tf_op jit(solution)/shard_map/all_gather | solution.py:19
  115.7 27.8 %copy-start.1 = (f32[2,64,512]{2,1,0:T(8,128)}, f32[2,64,512]{2,1,0:T(8,128)S(1)}, u32[]{:S(2)}) copy-start(f32[2,64,512]{2,1,0:T(8,128)S(1)} %fusion.5) | copy-start | bytes 786436
Sparse Core Ops, SparseCore 0:
  40.1 40.0 all-gather.2
where the time goes:
time: 151 us; the launch traced here: 150 us
  blocking collectives  63.2 us (42%)
  other arithmetic  32 us (21%)
  local copies, waits for them, and re-layouts  29.1 us (19%)
  between operations  14.4 us (10%)
  matrix products  11.7 us (8%)
    all_gather x2, blocking collectives, gather_turned(): filled, at, outs = (lax.all_gather(both, axis, axis=0, tiled=True), 0, [])  42.6 us
    unnamed x18, local copies, waits for them, and re-layouts  23.8 us
    all_gather x1, blocking collectives, body(): projected = lax.all_gather(projected_part, 'col', axis=2, tiled=True)  20.6 us
    another operation x4, other arithmetic, body(): basis = tri_solve(jnp.linalg.cholesky(gram), range_t)  11.9 us
    another operation x3, other arithmetic, tri_solve(): jax.scipy.linalg.solve_triangular(low, right, lower=True)  9.92 us
    dot_general x1, matrix products, body(): change = jnp.einsum('apbs,bsq->apbq', left, zcols, precision=highest)  6.7 us
    select_n x2, other arithmetic, pair_apply(): jnp.where(twin, (first_in * diag_two - second_in * offdiag) / determinant...  4.37 us
  transfers between devices with their start and end apart: 1, of which 0 were waited for; matrix products, arithmetic and copies ran while one was open for 20% of the time, Pallas kernels for 0%

commit v1 on v0

--- a/solution.py
+++ b/solution.py
@@ -82,7 +82,21 @@
     gram = jnp.einsum("arp,asp->ars", range_t, range_t, precision=highest) / width
     basis = tri_solve(jnp.linalg.cholesky(gram), range_t)
     projected_part = jnp.einsum("arp,apq->arq", basis, updated, precision=highest)
-    projected = lax.all_gather(projected_part, "col", axis=2, tiled=True)
+    ways, here, lap = (lax.axis_size("col"), lax.axis_index("col"), projected_part.shape[2])
+    lengths = [n * ways if d == 2 else n for d, n in enumerate(projected_part.shape)]
+    full = lax.dynamic_update_slice_in_dim(
+        jnp.zeros(lengths, projected_part.dtype), projected_part, here * lap, axis=2
+    )
+    going_up = going_down = projected_part
+    for far in range(1, ways // 2 + 1):
+        going_up = lax.ppermute(going_up, "col", [(d, (d + 1) % ways) for d in range(ways)])
+        full = lax.dynamic_update_slice_in_dim(full, going_up, (here - far) % ways * lap, axis=2)
+        if 2 * far < ways:
+            going_down = lax.ppermute(going_down, "col", [(d, (d - 1) % ways) for d in range(ways)])
+            full = lax.dynamic_update_slice_in_dim(
+                full, going_down, (here + far) % ways * lap, axis=2
+            )
+    projected = full
     permuted = jnp.take(projected, perm, axis=2)
     coeff = pair_apply(permuted, pair_kind, pivot_values) / jnp.sqrt(jnp.float32(width))
     return (trail_out, basis[:, None], coeff[:, None])

time: 151 us -> 170 us (1.13); the launches traced: 150 us -> 167 us
  starting transfers between devices: 0.04 us -> 23.9 us
  blocking collectives: 63.2 us -> 42.8 us
  waiting for transfers between devices: 0.04 us -> 13 us
    ppermute x0 -> x15, starting transfers between devices: none -> 23.8 us  [the longest x7 21.5 us: body(): lax.ppermute(going_down, 'col', [(d, (d - 1) % ways) for d in range(ways)])]
    all_gather x1 -> x0, blocking collectives: 20.6 us -> none  [body(): projected = lax.all_gather(projected_part, 'col', axis=2, tiled=True)]
    ppermute x0 -> x15, waiting for transfers between devices: none -> 12.9 us  [the longest x8 8.07 us: body(): lax.ppermute(going_up, 'col', [(d, (d + 1) % ways) for d in range(ways)])]
  transfers between devices with their start and end apart: 1 -> 16, of which waited for: 0 -> 8; matrix products, arithmetic and copies ran while one was open for 20% -> 19% of each run, Pallas kernels for 0% -> 0%
where the time goes in v1:
time: 170 us; the launch traced here: 167 us
  blocking collectives  42.8 us (25%)
  other arithmetic  31.7 us (19%)
  local copies, waits for them, and re-layouts  29.5 us (17%)
  starting transfers between devices  23.9 us (14%)
  between operations  14.7 us (9%)
  waiting for transfers between devices  13 us (8%)
  matrix products  11.6 us (7%)
    all_gather x2, blocking collectives, gather_turned(): filled, at, outs = (lax.all_gather(both, axis, axis=0, tiled=True), 0, [])  42.8 us
    unnamed x18, local copies, waits for them, and re-layouts  23.8 us
    ppermute x7, starting transfers between devices, body(): lax.ppermute(going_down, 'col', [(d, (d - 1) % ways) for d in range(ways)])  21.5 us
    another operation x4, other arithmetic, body(): basis = tri_solve(jnp.linalg.cholesky(gram), range_t)  11.9 us
    another operation x3, other arithmetic, tri_solve(): jax.scipy.linalg.solve_triangular(low, right, lower=True)  9.92 us
    ppermute x8, waiting for transfers between devices, body(): lax.ppermute(going_up, 'col', [(d, (d + 1) % ways) for d in range(ways)])  8.07 us
    dot_general x1, matrix products, body(): change = jnp.einsum('apbs,bsq->apbq', left, zcols, precision=highest)  6.69 us
    ppermute x7, waiting for transfers between devices, body(): lax.ppermute(going_down, 'col', [(d, (d - 1) % ways) for d in range(ways)])  4.85 us
  transfers between devices with their start and end apart: 16, of which 8 were waited for; matrix products, arithmetic and copies ran while one was open for 19% of the time, Pallas kernels for 0%

profile of v1, /device:TPU:1, one launch (start us, length us, event | category | flops | bytes accessed | tf_op | source)
XLA Modules:
  0.0 167.1 jit_solution(7907485998177092797)
XLA Ops:
  7.2 0.0 copy-start
  7.2 0.0 all-gather.3.cloned.1.call-start
  7.3 0.8 broadcast_compare_fusion
  8.0 0.8 fusion.11
  8.8 0.8 copy.122
  9.6 0.1 reshape.159
  9.7 0.8 copy.123
  10.5 0.1 reshape.160
  10.6 1.0 copy.129
  11.6 22.7 %all_gather.13 = f32[512,256]{1,0:T(8,128)S(1)} all-gather(f32[32,256]{1,0:T(8,128)S(1)} %pad_maximum_fusion.2), channel_id=1, replica_groups=mesh['row'=16,'col'=16] {'col'}, dimensions={0}, use_global_device_ids=true | all-gather | bytes 557056 | tf_op jit(solution)/shard_map/all_gather | solution.py:10
  34.4 0.1 copy.125
  34.6 0.1 copy.124
  34.7 2.2 %broadcast_select_fusion.4 = (f32[64,256,1]{0,2,1:T(1,128)S(1)}, f32[64,256,1]{0,2,1:T(1,128)S(1)}) fusion(pred[256]{0:T(512)(128)(4,1)S(1)} %broadcast_compare_fusion, f32[64,256,2]{0,2,1:T(2,128)S(1)} %bitcast.108, f32[256]{0:T(256)S(1)} %bitcast.120, f32[256]{0:T(256)S(1)} %bitcast.126, f32[256]{0:T(256)S(1)} %bitcast.123, f32[256]{0:T(256)S(1)} %bitcast.117), kind=kLoop, calls=%fused_computation.11 | loop fusion | flops 196608 | bytes 266496 | tf_op jit(solution)/shard_map/jit(_where)/select_n | solution.py:31
  36.9 0.3 pad_maximum_fusion
  37.2 0.5 fusion.1
  37.7 0.4 fusion.14
  38.1 0.4 convolution_bitcast_fusion.1
  38.5 0.3 convolution_subtract_fusion
  38.8 1.1 convolution_bitcast_fusion
  40.0 0.0 all-gather.3.cloned.1.call-update
  40.3 0.2 broadcast_in_dim.48
  40.5 0.1 reshape.156
  40.6 0.1 reshape.157
  40.7 20.0 %all_gather.12 = f32[512,256]{1,0:T(8,128)S(1)} all-gather(f32[32,256]{1,0:T(8,128)S(1)} %pad_maximum_fusion.1), channel_id=1, replica_groups=mesh['row'=16,'col'=16] {'row'}, dimensions={0}, use_global_device_ids=true | all-gather | bytes 557056 | tf_op jit(solution)/shard_map/all_gather | solution.py:10
  60.8 0.1 copy.126
  60.9 0.1 copy.121
  61.1 11.0 %copy.128 = f32[2,1,512,2,1,512]{2,5,0,3,4,1:T(8,128)} copy(f32[2,1,512,2,1,512]{5,4,3,2,1,0:T(1,128)} %param.12) | data formatting | bytes 8388608 | tf_op args[0]
  72.0 0.5 fusion.12
  72.6 0.6 fusion.13
  73.1 6.7 %bitcast_subtract_fusion = f32[2,1,512,2,1,512]{2,5,0,3,4,1:T(8,128)} fusion(f32[2,1,512,2,1,512]{2,5,0,3,4,1:T(8,128)} %copy.128, f32[2,64,512,1]{2,1,3,0:T(8,128)S(1)} %bitcast.109, f32[2,512,2,64]{1,3,0,2:T(8,128)S(1)} %fusion.13), kind=kOutput, calls=%fused_computation.1 | convolution fusion | flops 806354944 | bytes 9175040 | tf_op jit(solution)/shard_map/apbs,bsq->apbq/dot_general | solution.py:71
  79.8 10.9 %copy.150 = f32[2,1,512,2,1,512]{5,4,3,2,1,0:T(1,128)} copy(f32[2,1,512,2,1,512]{2,5,0,3,4,1:T(8,128)} %bitcast_subtract_fusion) | data formatting | bytes 8388608
  90.8 0.0 all-gather.3.cloned.1.call-done
  90.8 2.6 %reduce_sum.9 = f32[2,64,512]{2,1,0:T(8,128)S(1)} reduce(f32[16,2,64,512]{3,2,1,0:T(8,128)} %bitcast.100, f32[]{:T(128)} %constant.152.clone.1), dimensions={0}, to_apply=%region_0.1 | reduce | flops 983040 | bytes 4456452 | tf_op jit(solution)/shard_map/reduce_sum | solution.py:19
  93.4 0.4 fusion.15
  93.8 0.1 copy.131
  93.9 11.7 %custom-call.8 = f32[2,64,64]{2,1,0:T(8,128)S(1)} custom-call(f32[2,64,64]{2,1,0:T(8,128)S(1)} %fusion.7), custom_call_target="Cholesky" | custom-call | tf_op jit(solution)/shard_map/jit(cholesky)/cholesky | solution.py:83
  105.7 0.1 compare_reduce_fusion
  105.8 0.1 select_bitcast_fusion
  105.9 9.8 %custom-call.9 = f32[2,1,64,64]{2,3,1,0:T(8,128)S(1)} custom-call(f32[2,1,64,64]{3,2,1,0:T(8,128)S(1)} %select_bitcast_fusion), custom_call_target="InvertDiagBlocksLowerTriangular" | custom-call | tf_op jit(solution)/shard_map/vmap(jit(_solve_triangular))/triangular_solve | solution.py:41
  115.7 0.4 fusion.5
  116.2 0.3 fusion.16
  116.5 4.9 %collective-permute-start.1 = (f32[2,64,32]{1,2,0:T(8,128)S(1)}, f32[2,64,32]{1,2,0:T(8,128)S(1)}, u32[]{:S(2)}, u32[]{:S(2)}) collective-permute-start(f32[2,64,32]{1,2,0:T(8,128)S(1)} %fusion.16), channel_id=1, source_target_pairs={{0,15},{1,0},{2,1},{3,2},{4,3},{5,4},{6,5},{7,6},{8,7},{9,8},{10,9... | collective-permute-start | bytes 49160 | tf_op jit(solution)/shard_map/ppermute | solution.py:95
  121.4 0.1 broadcast_in_dim.50
  121.6 0.8 collective-permute-done.1
  122.4 0.6 collective-permute-start.3
  123.0 1.7 %collective-permute-start.2 = (f32[2,64,32]{1,2,0:T(8,128)S(1)}, f32[2,64,32]{1,2,0:T(8,128)S(1)}, u32[]{:S(2)}, u32[]{:S(2)}) collective-permute-start(f32[2,64,32]{1,2,0:T(8,128)S(1)} %collective-permute-done), channel_id=1, source_target_pairs={{0,1},{1,2},{2,3},{3,4},{4,5},{5,6},{6,7},{7,8},{8,9},{9,10},{10,1... | collective-permute-start | bytes 49160 | tf_op jit(solution)/shard_map/ppermute | solution.py:92
  124.8 0.9 collective-permute-done.3
  125.7 1.9 %collective-permute-start.5 = (f32[2,64,32]{1,2,0:T(8,128)S(1)}, f32[2,64,32]{1,2,0:T(8,128)S(1)}, u32[]{:S(2)}, u32[]{:S(2)}) collective-permute-start(f32[2,64,32]{1,2,0:T(8,128)S(1)} %collective-permute-done.3), channel_id=1, source_target_pairs={{0,15},{1,0},{2,1},{3,2},{4,3},{5,4},{6,5},{7,6},{8,7},{9,8},{10,9... | collective-permute-start | bytes 49160 | tf_op jit(solution)/shard_map/ppermute | solution.py:95
  127.6 0.5 collective-permute-start.4
  128.2 0.9 collective-permute-done.5
  129.0 3.1 %collective-permute-start.7 = (f32[2,64,32]{1,2,0:T(8,128)S(1)}, f32[2,64,32]{1,2,0:T(8,128)S(1)}, u32[]{:S(2)}, u32[]{:S(2)}) collective-permute-start(f32[2,64,32]{1,2,0:T(8,128)S(1)} %collective-permute-done.5), channel_id=1, source_target_pairs={{0,15},{1,0},{2,1},{3,2},{4,3},{5,4},{6,5},{7,6},{8,7},{9,8},{10,9... | collective-permute-start | bytes 49160 | tf_op jit(solution)/shard_map/ppermute | solution.py:95
  132.2 0.8 collective-permute-done.7
  133.0 3.7 %collective-permute-start.9 = (f32[2,64,32]{1,2,0:T(8,128)S(1)}, f32[2,64,32]{1,2,0:T(8,128)S(1)}, u32[]{:S(2)}, u32[]{:S(2)}) collective-permute-start(f32[2,64,32]{1,2,0:T(8,128)S(1)} %collective-permute-done.7), channel_id=1, source_target_pairs={{0,15},{1,0},{2,1},{3,2},{4,3},{5,4},{6,5},{7,6},{8,7},{9,8},{10,9... | collective-permute-start | bytes 49160 | tf_op jit(solution)/shard_map/ppermute | solution.py:95
  136.8 0.8 collective-permute-done.9
  137.5 3.7 %collective-permute-start.11 = (f32[2,64,32]{1,2,0:T(8,128)S(1)}, f32[2,64,32]{1,2,0:T(8,128)S(1)}, u32[]{:S(2)}, u32[]{:S(2)}) collective-permute-start(f32[2,64,32]{1,2,0:T(8,128)S(1)} %collective-permute-done.9), channel_id=1, source_target_pairs={{0,15},{1,0},{2,1},{3,2},{4,3},{5,4},{6,5},{7,6},{8,7},{9,8},{10,9... | collective-permute-start | bytes 49160 | tf_op jit(solution)/shard_map/ppermute | solution.py:95
  141.3 0.8 collective-permute-done.11
  142.1 3.7 %collective-permute-start.13 = (f32[2,64,32]{1,2,0:T(8,128)S(1)}, f32[2,64,32]{1,2,0:T(8,128)S(1)}, u32[]{:S(2)}, u32[]{:S(2)}) collective-permute-start(f32[2,64,32]{1,2,0:T(8,128)S(1)} %collective-permute-done.11), channel_id=1, source_target_pairs={{0,15},{1,0},{2,1},{3,2},{4,3},{5,4},{6,5},{7,6},{8,7},{9,8},{10,9... | collective-permute-start | bytes 49160 | tf_op jit(solution)/shard_map/ppermute | solution.py:95
  145.9 3.6 %collective-permute-done.12 = f32[2,64,32]{1,2,0:T(8,128)S(1)} collective-permute-done((f32[2,64,32]{1,2,0:T(8,128)S(1)}, f32[2,64,32]{1,2,0:T(8,128)S(1)}, u32[]{:S(2)}, u32[]{:S(2)}) %collective-permute-start.12) | collective-permute-done | bytes 16416 | tf_op jit(solution)/shard_map/ppermute | solution.py:92
  149.5 4.5 %collective-permute-done.14 = f32[2,64,32]{1,2,0:T(8,128)S(1)} collective-permute-done((f32[2,64,32]{1,2,0:T(8,128)S(1)}, f32[2,64,32]{1,2,0:T(8,128)S(1)}, u32[]{:S(2)}, u32[]{:S(2)}) %collective-permute-start.14) | collective-permute-done | bytes 16416 | tf_op jit(solution)/shard_map/ppermute | solution.py:92
  154.0 2.1 %gather_fusion = f32[512,2,64]{2,1,0:T(2,128)S(1)} fusion(f32[2,64,512]{1,0,2:T(2,128)S(1)} %copy_dynamic-update-slice_fusion, s32[1024]{0:T(1024)S(1)} %pad_clamp_fusion), kind=kCustom, calls=%fused_computation | custom fusion | bytes 526336 | tf_op jit(solution)/shard_map/jit(_take)/gather | solution.py:100
  156.2 0.4 broadcast_select_fusion.2
  156.5 2.2 %broadcast_select_fusion.1 = (f32[2,64,256,1]{1,3,2,0:T(1,128)S(1)}, f32[2,64,256,1]{1,3,2,0:T(1,128)S(1)}) fusion(pred[256]{0:T(512)(128)(4,1)S(1)} %broadcast_compare_fusion, f32[2,64,256,2]{1,3,2,0:T(2,128)S(1)} %broadcast_select_fusion.2, f32[256]{0:T(256)S(1)} %bitcast.122, f32[256]{0:T(256)S(1)} %multiply_subtract_fusion, f32[256]{0:T(256)S(1)} %bitcast.125, ...), kind=kLoop, calls=%fused_computation.7 | loop fusion | flops 393216 | bytes 528640 | tf_op jit(solution)/shard_map/jit(_where)/select_n | solution.py:31
  158.7 0.6 maximum_multiply_fusion
  159.4 0.9 copy.152
  (58 shorter events, 0.9 us)
Async XLA Ops:
  7.2 30.0 %copy-start = (f32[64,512]{1,0:T(8,128)S(1)}, f32[64,512]{1,0:T(8,128)}, u32[]{:S(2)}) copy-start(f32[64,512]{1,0:T(8,128)} %param.19) | copy-start | bytes 393220
  7.2 30.9 %copy-start.5 = (s32[512]{0:T(512)S(1)}, s32[512]{0:T(512)}, u32[]{:S(2)}) copy-start(s32[512]{0:T(512)} %param.21) | copy-start | bytes 6148
  7.2 31.3 %copy-start.6 = (f32[64,32]{0,1:T(8,128)S(1)}, f32[64,32]{0,1:T(8,128)}, u32[]{:S(2)}) copy-start(f32[64,32]{0,1:T(8,128)} %param.18) | copy-start | bytes 24580
  7.2 31.3 %copy-start.2 = (f32[2,1,512,32]{2,3,1,0:T(8,128)S(1)}, f32[2,1,512,32]{2,3,1,0:T(8,128)}, u32[]{:S(2)}) copy-start(f32[2,1,512,32]{2,3,1,0:T(8,128)} %param.13) | copy-start | bytes 393220
  7.2 33.2 %copy-start.3 = (f32[2,1,64,32]{2,3,1,0:T(8,128)S(1)}, f32[2,1,64,32]{2,3,1,0:T(8,128)}, u32[]{:S(2)}) copy-start(f32[2,1,64,32]{2,3,1,0:T(8,128)} %param.16) | copy-start | bytes 49156
  7.2 33.4 %copy-start.4 = (f32[2,1,64,32]{2,3,1,0:T(8,128)S(1)}, f32[2,1,64,32]{2,3,1,0:T(8,128)}, u32[]{:S(2)}) copy-start(f32[2,1,64,32]{2,3,1,0:T(8,128)} %param.17) | copy-start | bytes 49156
  7.2 83.6 %all-gather.3.cloned.1.call-start = ((), (), s32[]{:S(2)}) async-start(), calls=%async_computation | async-start | bytes 4456448 | tf_op jit(solution)/shard_map/all_gather | solution.py:19
  116.1 44.1 %copy-start.1 = (f32[2,64,512]{2,1,0:T(8,128)}, f32[2,64,512]{2,1,0:T(8,128)S(1)}, u32[]{:S(2)}) copy-start(f32[2,64,512]{2,1,0:T(8,128)S(1)} %fusion.5) | copy-start | bytes 786436
  116.5 5.9 %collective-permute-start.1 = (f32[2,64,32]{1,2,0:T(8,128)S(1)}, f32[2,64,32]{1,2,0:T(8,128)S(1)}, u32[]{:S(2)}, u32[]{:S(2)}) collective-permute-start(f32[2,64,32]{1,2,0:T(8,128)S(1)} %fusion.16), channel_id=1, source_target_pairs={{0,15},{1,0},{2,1},{3,2},{4,3},{5,4},{6,5},{7,6},{8,7},{9,8},{10,9... | collective-permute-start | bytes 49160 | tf_op jit(solution)/shard_map/ppermute | solution.py:95
  121.4 1.6 collective-permute-start
  122.4 3.3 %collective-permute-start.3 = (f32[2,64,32]{1,2,0:T(8,128)S(1)}, f32[2,64,32]{1,2,0:T(8,128)S(1)}, u32[]{:S(2)}, u32[]{:S(2)}) collective-permute-start(f32[2,64,32]{1,2,0:T(8,128)S(1)} %collective-permute-done.1), channel_id=1, source_target_pairs={{0,15},{1,0},{2,1},{3,2},{4,3},{5,4},{6,5},{7,6},{8,7},{9,8},{10,9... | collective-permute-start | bytes 49160 | tf_op jit(solution)/shard_map/ppermute | solution.py:95
  123.0 4.6 %collective-permute-start.2 = (f32[2,64,32]{1,2,0:T(8,128)S(1)}, f32[2,64,32]{1,2,0:T(8,128)S(1)}, u32[]{:S(2)}, u32[]{:S(2)}) collective-permute-start(f32[2,64,32]{1,2,0:T(8,128)S(1)} %collective-permute-done), channel_id=1, source_target_pairs={{0,1},{1,2},{2,3},{3,4},{4,5},{5,6},{6,7},{7,8},{8,9},{9,10},{10,1... | collective-permute-start | bytes 49160 | tf_op jit(solution)/shard_map/ppermute | solution.py:92
  125.7 3.3 %collective-permute-start.5 = (f32[2,64,32]{1,2,0:T(8,128)S(1)}, f32[2,64,32]{1,2,0:T(8,128)S(1)}, u32[]{:S(2)}, u32[]{:S(2)}) collective-permute-start(f32[2,64,32]{1,2,0:T(8,128)S(1)} %collective-permute-done.3), channel_id=1, source_target_pairs={{0,15},{1,0},{2,1},{3,2},{4,3},{5,4},{6,5},{7,6},{8,7},{9,8},{10,9... | collective-permute-start | bytes 49160 | tf_op jit(solution)/shard_map/ppermute | solution.py:95
  127.6 4.6 %collective-permute-start.4 = (f32[2,64,32]{1,2,0:T(8,128)S(1)}, f32[2,64,32]{1,2,0:T(8,128)S(1)}, u32[]{:S(2)}, u32[]{:S(2)}) collective-permute-start(f32[2,64,32]{1,2,0:T(8,128)S(1)} %collective-permute-done.2), channel_id=1, source_target_pairs={{0,1},{1,2},{2,3},{3,4},{4,5},{5,6},{6,7},{7,8},{8,9},{9,10},{10,1... | collective-permute-start | bytes 49160 | tf_op jit(solution)/shard_map/ppermute | solution.py:92
  129.0 3.9 %collective-permute-start.7 = (f32[2,64,32]{1,2,0:T(8,128)S(1)}, f32[2,64,32]{1,2,0:T(8,128)S(1)}, u32[]{:S(2)}, u32[]{:S(2)}) collective-permute-start(f32[2,64,32]{1,2,0:T(8,128)S(1)} %collective-permute-done.5), channel_id=1, source_target_pairs={{0,15},{1,0},{2,1},{3,2},{4,3},{5,4},{6,5},{7,6},{8,7},{9,8},{10,9... | collective-permute-start | bytes 49160 | tf_op jit(solution)/shard_map/ppermute | solution.py:95
  132.1 4.6 %collective-permute-start.6 = (f32[2,64,32]{1,2,0:T(8,128)S(1)}, f32[2,64,32]{1,2,0:T(8,128)S(1)}, u32[]{:S(2)}, u32[]{:S(2)}) collective-permute-start(f32[2,64,32]{1,2,0:T(8,128)S(1)} %collective-permute-done.4), channel_id=1, source_target_pairs={{0,1},{1,2},{2,3},{3,4},{4,5},{5,6},{6,7},{7,8},{8,9},{9,10},{10,1... | collective-permute-start | bytes 49160 | tf_op jit(solution)/shard_map/ppermute | solution.py:92
  133.0 4.6 %collective-permute-start.9 = (f32[2,64,32]{1,2,0:T(8,128)S(1)}, f32[2,64,32]{1,2,0:T(8,128)S(1)}, u32[]{:S(2)}, u32[]{:S(2)}) collective-permute-start(f32[2,64,32]{1,2,0:T(8,128)S(1)} %collective-permute-done.7), channel_id=1, source_target_pairs={{0,15},{1,0},{2,1},{3,2},{4,3},{5,4},{6,5},{7,6},{8,7},{9,8},{10,9... | collective-permute-start | bytes 49160 | tf_op jit(solution)/shard_map/ppermute | solution.py:95
  136.7 4.6 %collective-permute-start.8 = (f32[2,64,32]{1,2,0:T(8,128)S(1)}, f32[2,64,32]{1,2,0:T(8,128)S(1)}, u32[]{:S(2)}, u32[]{:S(2)}) collective-permute-start(f32[2,64,32]{1,2,0:T(8,128)S(1)} %collective-permute-done.6), channel_id=1, source_target_pairs={{0,1},{1,2},{2,3},{3,4},{4,5},{5,6},{6,7},{7,8},{8,9},{9,10},{10,1... | collective-permute-start | bytes 49160 | tf_op jit(solution)/shard_map/ppermute | solution.py:92
  137.5 4.6 %collective-permute-start.11 = (f32[2,64,32]{1,2,0:T(8,128)S(1)}, f32[2,64,32]{1,2,0:T(8,128)S(1)}, u32[]{:S(2)}, u32[]{:S(2)}) collective-permute-start(f32[2,64,32]{1,2,0:T(8,128)S(1)} %collective-permute-done.9), channel_id=1, source_target_pairs={{0,15},{1,0},{2,1},{3,2},{4,3},{5,4},{6,5},{7,6},{8,7},{9,8},{10,9... | collective-permute-start | bytes 49160 | tf_op jit(solution)/shard_map/ppermute | solution.py:95
  141.2 4.6 %collective-permute-start.10 = (f32[2,64,32]{1,2,0:T(8,128)S(1)}, f32[2,64,32]{1,2,0:T(8,128)S(1)}, u32[]{:S(2)}, u32[]{:S(2)}) collective-permute-start(f32[2,64,32]{1,2,0:T(8,128)S(1)} %collective-permute-done.8), channel_id=1, source_target_pairs={{0,1},{1,2},{2,3},{3,4},{4,5},{5,6},{6,7},{7,8},{8,9},{9,10},{10,1... | collective-permute-start | bytes 49160 | tf_op jit(solution)/shard_map/ppermute | solution.py:92
  142.1 7.4 %collective-permute-start.13 = (f32[2,64,32]{1,2,0:T(8,128)S(1)}, f32[2,64,32]{1,2,0:T(8,128)S(1)}, u32[]{:S(2)}, u32[]{:S(2)}) collective-permute-start(f32[2,64,32]{1,2,0:T(8,128)S(1)} %collective-permute-done.11), channel_id=1, source_target_pairs={{0,15},{1,0},{2,1},{3,2},{4,3},{5,4},{6,5},{7,6},{8,7},{9,8},{10,9... | collective-permute-start | bytes 49160 | tf_op jit(solution)/shard_map/ppermute | solution.py:95
  145.8 3.7 %collective-permute-start.12 = (f32[2,64,32]{1,2,0:T(8,128)S(1)}, f32[2,64,32]{1,2,0:T(8,128)S(1)}, u32[]{:S(2)}, u32[]{:S(2)}) collective-permute-start(f32[2,64,32]{1,2,0:T(8,128)S(1)} %collective-permute-done.10), channel_id=1, source_target_pairs={{0,1},{1,2},{2,3},{3,4},{4,5},{5,6},{6,7},{7,8},{8,9},{9,10},{10,1... | collective-permute-start | bytes 49160 | tf_op jit(solution)/shard_map/ppermute | solution.py:92
  149.4 4.6 %collective-permute-start.14 = (f32[2,64,32]{1,2,0:T(8,128)S(1)}, f32[2,64,32]{1,2,0:T(8,128)S(1)}, u32[]{:S(2)}, u32[]{:S(2)}) collective-permute-start(f32[2,64,32]{1,2,0:T(8,128)S(1)} %collective-permute-done.12), channel_id=1, source_target_pairs={{0,1},{1,2},{2,3},{3,4},{4,5},{5,6},{6,7},{7,8},{8,9},{9,10},{10,1... | collective-permute-start | bytes 49160 | tf_op jit(solution)/shard_map/ppermute | solution.py:92
Sparse Core Ops, SparseCore 0:
  40.1 40.0 all-gather.2
